TPU v7x, 32 devices: a whole 2x2x4 slice. The times are simulated.
32 devices in a mesh: grp: 4 (over z), dev: 8 (over y, x, core).
Axes of the slice: x: 2, y: 2, z: 4, core: 2. Of those that a mesh axis runs over, the one named last changes fastest.
Arguments:
- blocks: bfloat16 [4096, 128, 128], P(('grp', 'dev')), may hold values from -0.29882812 to 0.29882812
- ids_one: int32 [2, 4096], P(None, ('grp', 'dev')), may hold values from 0 to 255, as said below
- ids_two: int32 [2, 2048], P(None, ('grp', 'dev')), may hold values from 0 to 127, as said below
- ids_three: int32 [2, 1024], P(None, ('grp', 'dev')), may hold values from 0 to 63
- match_one: int32 [256, 128], replicated, may hold values from 0 to 127, as said below
- match_two: int32 [128, 128], replicated, may hold values from 0 to 127, as said below
- match_three: int32 [64, 128], replicated, may hold values from 0 to 127, as said below
- target_one: int32 [4096], P(('grp', 'dev')), may hold values from 0 to 63
- target_two: int32 [2048], P(('grp', 'dev')), may hold values from 0 to 31
- target_three: int32 [1024], P(('grp', 'dev')), may hold values from 0 to 15
- vertex_weights: float32 [256, 128], P(('grp', 'dev')), may hold values from 0.1 to 120, as said below
Outputs:
- coarse_graph: float32 [512, 128, 128], P(('grp', 'dev'))
- rel_weight: float32 [32, 128], P(('grp', 'dev'))
Inputs may be any that keep to these rules, and one draw needn't show every extreme that they name: `match_one`: rows 2b and 2b + 1 together name every number 0 to 127 exactly twice. `match_two`: rows 2b and 2b + 1 together name every number 0 to 127 exactly twice. `match_three`: rows 2b and 2b + 1 together name every number 0 to 127 exactly twice. `ids_one`: a fine block's row and column vertex blocks, halved by integer division, are the ids_two of the coarse slot it goes to. `ids_two`: a first-level block's row and column vertex blocks, halved by integer division, are the ids_three of the coarse slot it goes to. `vertex_weights`: positive.
All inputs are finite; a program needn't handle non-finite values.
Results may differ from a plain program's by a relative error of at most 0.0003.
Values may be sent and summed in bfloat16 or wider, within the bound.
No kernel may reach another device: no remote copies, remote signals or barrier semaphores. Data moves between devices by JAX's collectives and lax.ppermute only.
A program may use at most 128 MiB of HBM per device.

v0:
```python
import math

import jax
import jax.numpy as jnp
from jax import lax
from jax.sharding import PartitionSpec as P


def project(blocks, pair_ids, table):
    row_map = table[pair_ids[0]]
    col_map = table[pair_ids[1]]
    count = blocks.shape[0]
    width = blocks.shape[1]
    group = math.gcd(count, 32)
    lanes = jnp.arange(width, dtype=jnp.int32)
    narrow = blocks.dtype == jnp.bfloat16

    def single(piece):
        block_part, rows_part, cols_part = piece
        right_hot = (cols_part[:, :, None] == lanes).astype(jnp.float32)
        if narrow:
            left_hot = (rows_part[:, :, None] == lanes).astype(jnp.bfloat16)
            halfway = jnp.einsum(
                "gim,gij->gmj", left_hot, block_part, preferred_element_type=jnp.float32
            )
        else:
            left_hot = (rows_part[:, :, None] == lanes).astype(jnp.float32)
            halfway = jnp.einsum(
                "gim,gij->gmj",
                left_hot,
                block_part,
                preferred_element_type=jnp.float32,
                precision=lax.Precision.HIGHEST,
            )
        return jnp.einsum(
            "gmj,gjn->gmn",
            halfway,
            right_hot,
            preferred_element_type=jnp.float32,
            precision=lax.Precision.HIGHEST,
        )

    pieces = (
        blocks.reshape(count // group, group, width, width),
        row_map.reshape(count // group, group, width),
        col_map.reshape(count // group, group, width),
    )
    return lax.map(single, pieces).reshape(count, width, width)


def gather_sum(received, targets, count):
    width = received.shape[1]
    hot = (jnp.arange(count, dtype=jnp.int32)[:, None] == targets[None, :]).astype(jnp.float32)
    flat = jnp.dot(
        hot,
        received.reshape(received.shape[0], width * width),
        preferred_element_type=jnp.float32,
        precision=lax.Precision.HIGHEST,
    )
    return flat.reshape(count, width, width)


def pair_weights(weights, table_rows):
    count, width = weights.shape
    lanes = jnp.arange(width, dtype=jnp.int32)
    hot = (table_rows.reshape(count // 2, 2 * width)[:, :, None] == lanes).astype(jnp.float32)
    return jnp.einsum(
        "kj,kjm->km",
        weights.reshape(count // 2, 2 * width),
        hot,
        preferred_element_type=jnp.float32,
        precision=lax.Precision.HIGHEST,
    )


def per_device(
    blocks,
    ids_one,
    ids_two,
    ids_three,
    match_one,
    match_two,
    match_three,
    target_one,
    target_two,
    target_three,
    vertex_weights,
):
    slots_zero = blocks.shape[0]
    labels = jnp.stack([ids_one[0], ids_one[1], target_one], axis=1)
    fine_in, labels_in = (
        lax.all_to_all(blocks, "dev", split_axis=0, concat_axis=0, tiled=True),
        lax.all_to_all(labels, "dev", split_axis=0, concat_axis=0, tiled=True),
    )
    received = project(fine_in, labels_in[:, :2].T, match_one)
    arrived = labels_in[:, 2]
    coarse_one = gather_sum(received, arrived, slots_zero // 2)
    parts_two = project(coarse_one, ids_two, match_two)
    received_two, arrived_two = (
        lax.all_to_all(parts_two, "dev", split_axis=0, concat_axis=0, tiled=True),
        lax.all_to_all(target_two, "dev", split_axis=0, concat_axis=0, tiled=True),
    )
    coarse_two = gather_sum(received_two, arrived_two, slots_zero // 4)
    parts_three = project(coarse_two, ids_three, match_three)
    received_three, arrived_three = (
        lax.all_to_all(parts_three, "grp", split_axis=0, concat_axis=0, tiled=True),
        lax.all_to_all(target_three, "grp", split_axis=0, concat_axis=0, tiled=True),
    )
    coarse_graph = gather_sum(received_three, arrived_three, slots_zero // 8)
    total = lax.psum(jnp.sum(vertex_weights), ("grp", "dev"))
    owned = vertex_weights.shape[0]
    position = lax.axis_index(("grp", "dev"))
    rows_one = lax.dynamic_slice_in_dim(match_one, position * owned, owned, 0)
    weights_one = pair_weights(vertex_weights, rows_one)
    rows_two = lax.dynamic_slice_in_dim(match_two, position * (owned // 2), owned // 2, 0)
    weights_two = pair_weights(weights_one, rows_two)
    rows_three = lax.dynamic_slice_in_dim(match_three, position * (owned // 4), owned // 4, 0)
    weights_three = pair_weights(weights_two, rows_three)
    vertices = weights_three.shape[0] * lax.axis_size(("grp", "dev")) * weights_three.shape[1]
    rel_weight = weights_three * vertices / total
    return (coarse_graph, rel_weight)


def solution(mesh):
    return jax.shard_map(
        per_device,
        mesh=mesh,
        in_specs=(
            P(("grp", "dev"), None, None),
            P(None, ("grp", "dev")),
            P(None, ("grp", "dev")),
            P(None, ("grp", "dev")),
            P(),
            P(),
            P(),
            P(("grp", "dev")),
            P(("grp", "dev")),
            P(("grp", "dev")),
            P(("grp", "dev"), None),
        ),
        out_specs=(P(("grp", "dev"), None, None), P(("grp", "dev"), None)),
        check_vma=False,
    )
```

profile of v0, /device:TPU:0, one launch (start us, length us, event | category | flops | bytes accessed | tf_op | source)
XLA Modules:
  0.0 287.6 jit_solution(8036044374910287233)
XLA Ops:
  2.3 9.8 %all_to_all.42 = s32[8,16,3]{1,2,0:T(4,128)S(1)} all-to-all(s32[8,16,3]{1,2,0:T(4,128)S(1)} %copy.34), channel_id=1, replica_groups=mesh['grp'=4,'dev'=8] {'dev'}, dimensions={0} | all-to-all | bytes 3072 | tf_op jit(solution)/shard_map/all_to_all | solution.py:93
  12.1 4.7 %all-to-all-start.3 = ((bf16[128,128,128]{2,1,0:T(8,128)(2,1)}), bf16[128,128,128]{2,1,0:T(8,128)(2,1)}, u32[]{:S(2)}, u32[]{:S(2)}) async-start(bf16[128,128,128]{2,1,0:T(8,128)(2,1)} %param.15), calls=%async_computation.3 | async-start | bytes 8388608 | tf_op jit(solution)/shard_map/all_to_all | solution.py:92
  20.2 45.7 %all-to-all-done.3 = bf16[128,128,128]{2,1,0:T(8,128)(2,1)} async-done(((bf16[128,128,128]{2,1,0:T(8,128)(2,1)}), bf16[128,128,128]{2,1,0:T(8,128)(2,1)}, u32[]{:S(2)}, u32[]{:S(2)}) %all-to-all-start.3) | async-done | bytes 4194336 | tf_op jit(solution)/shard_map/all_to_all | solution.py:92
  65.9 3.3 %all-to-all-start.1 = ((s32[8,8,1]{1,2,0:T(1,128)}), s32[8,8,1]{1,2,0:T(1,128)S(1)}, u32[]{:S(2)}, u32[]{:S(2)}) async-start(s32[8,8,1]{1,2,0:T(1,128)} %bitcast.4), calls=%async_computation.1 | async-start | bytes 8192 | tf_op jit(solution)/shard_map/all_to_all | solution.py:101
  69.2 21.0 %while.28 = (s32[]{:T(128)}, f32[4,32,128,128]{3,2,1,0:T(8,128)}, s32[4,32,128]{2,1,0:T(8,128)S(1)}, bf16[4,32,128,128]{3,2,1,0:T(8,128)(2,1)}, s32[4,32,128]{2,1,0:T(8,128)S(1)}, /*index=5*/s32[]{:T(128)}) while((s32[]{:T(128)}, f32[4,32,128,128]{3,2,1,0:T(8,128)}, s32[4,32,128]{2,1,0:T(8,128)S(1)}, ...), condition=%wide.region_1.2_spmd.clone.clone, body=%wide.region_0.1_spmd.clone.clone.sunk | while | flops 940572672 | bytes 7439433 | solution.py:48
  69.3 2.6 fusion.66
  71.9 2.7 bitcast_dynamic-update-slice_fusion.4
  74.5 2.6 fusion.66
  77.1 2.6 bitcast_dynamic-update-slice_fusion.4
  79.7 2.6 fusion.66
  82.3 2.7 bitcast_dynamic-update-slice_fusion.4
  85.0 2.6 fusion.66
  87.5 2.7 bitcast_dynamic-update-slice_fusion.4
  90.2 13.2 %copy.74 = f32[16,8,128,128]{3,1,2,0:T(8,128)} copy(f32[16,8,128,128]{3,2,1,0:T(8,128)} %bitcast.158) | data formatting | bytes 16777216
  103.4 9.0 %copy.36 = f32[16384,128]{1,0:T(8,128)} copy(f32[16384,128]{0,1:T(8,128)} %bitcast.157) | data formatting | bytes 16777216 | tf_op jit(solution)/shard_map/dot_general | solution.py:54
  112.4 10.4 %fusion.35 = f32[2,32,128,128]{3,1,2,0:T(8,128)} fusion(f32[128,128,128,1]{2,1,0,3:T(8,128)} %bitcast.156, s32[128]{0:T(128)S(1)} %slice_bitcast_fusion.1, s32[2,32]{1,0:T(2,128)S(1)} %multiply_add_fusion), kind=kOutput, calls=%fused_computation.60 | convolution fusion | flops 1610620928 | bytes 12583680 | tf_op jit(solution)/shard_map/dot_general | solution.py:54
  122.7 17.3 %while.29 = (s32[]{:T(128)}, f32[2,32,128,128]{3,2,1,0:T(8,128)}, s32[2,32,128]{2,1,0:T(8,128)S(1)}, f32[2,32,128,128]{3,1,2,0:T(8,128)}, s32[2,32,128]{2,1,0:T(8,128)S(1)}, /*index=5*/s32[]{:T(128)}) while((s32[]{:T(128)}, f32[2,32,128,128]{3,2,1,0:T(8,128)}, s32[2,32,128]{2,1,0:T(8,128)S(1)}, ...), condition=%wide.region_3.4_spmd.clone.clone, body=%wide.region_2.3_spmd.clone.clone.sunk | while | flops 1611661312 | bytes 12681805 | solution.py:48
  122.7 1.8 constant_dynamic-slice_fusion.4
  124.5 4.2 %fusion.68 = f32[32,128,128]{2,1,0:T(8,128)S(1)} fusion(f32[1,32,128,128]{3,1,2,0:T(8,128)S(1)} %constant_dynamic-slice_fusion.4, s32[32,128]{1,0:T(8,128)S(1)} %get-tuple-element.280), kind=kOutput, calls=%fused_computation.23.clone.1 | convolution fusion | flops 805830656 | bytes 4210688 | tf_op jit(solution)/shard_map/while/body/eval_jaxpr/gim,gij->gmj/dot_general | solution.py:28
  128.7 2.7 bitcast_dynamic-update-slice_fusion.5
  131.4 1.8 constant_dynamic-slice_fusion.4
  133.2 4.2 %fusion.68 = f32[32,128,128]{2,1,0:T(8,128)S(1)} fusion(f32[1,32,128,128]{3,1,2,0:T(8,128)S(1)} %constant_dynamic-slice_fusion.4, s32[32,128]{1,0:T(8,128)S(1)} %get-tuple-element.280), kind=kOutput, calls=%fused_computation.23.clone.1 | convolution fusion | flops 805830656 | bytes 4210688 | tf_op jit(solution)/shard_map/while/body/eval_jaxpr/gim,gij->gmj/dot_general | solution.py:28
  137.4 2.6 bitcast_dynamic-update-slice_fusion.5
  140.1 4.7 %all-to-all-start.4 = ((f32[64,128,128]{2,1,0:T(8,128)}), f32[64,128,128]{2,1,0:T(8,128)}, u32[]{:S(2)}, u32[]{:S(2)}) async-start(f32[64,128,128]{2,1,0:T(8,128)} %bitcast.26), calls=%async_computation.4 | async-start | bytes 8388608 | tf_op jit(solution)/shard_map/all_to_all | solution.py:100
  148.0 45.9 %all-to-all-done.4 = f32[64,128,128]{2,1,0:T(8,128)} async-done(((f32[64,128,128]{2,1,0:T(8,128)}), f32[64,128,128]{2,1,0:T(8,128)}, u32[]{:S(2)}, u32[]{:S(2)}) %all-to-all-start.4) | async-done | bytes 4194336 | tf_op jit(solution)/shard_map/all_to_all | solution.py:100
  193.9 4.9 %all-to-all-start = ((s32[4,8,1]{1,2,0:T(1,128)}), s32[4,8,1]{1,2,0:T(1,128)S(1)}, u32[]{:S(2)}, u32[]{:S(2)}) async-start(s32[4,8,1]{1,2,0:T(1,128)} %bitcast), calls=%async_computation | async-start | bytes 4096 | tf_op jit(solution)/shard_map/all_to_all | solution.py:107
  198.8 6.1 %fusion.15 = f32[32,128,128]{2,0,1:T(8,128)S(1)} fusion(s32[64]{0:T(128)S(1)} %eq.224, f32[8,8,128,128]{3,2,1,0:T(8,128)} %bitcast.64), kind=kOutput, calls=%fused_computation.33 | convolution fusion | flops 402655232 | bytes 6291712 | tf_op jit(solution)/shard_map/dot_general | solution.py:54
  204.8 2.6 fusion.21
  207.4 2.7 fusion.23
  210.1 5.2 %all-to-all-start.5 = ((f32[32,128,128]{2,1,0:T(8,128)}), f32[32,128,128]{2,1,0:T(8,128)S(1)}, u32[]{:S(2)}, u32[]{:S(2)}) async-start(f32[32,128,128]{2,1,0:T(8,128)} %fusion.23), calls=%async_computation.5 | async-start | bytes 4194304 | tf_op jit(solution)/shard_map/all_to_all | solution.py:106
  215.9 65.5 %psum.7 = f32[]{:T(128)} all-reduce(f32[]{:T(128)} %reduce_sum.9), channel_id=1, replica_groups=mesh['grp'=4,'dev'=8] {'grp','dev'}, use_global_device_ids=true, to_apply=%region_5.6 | all-reduce | flops 1 | bytes 8 | tf_op jit(solution)/shard_map/psum | solution.py:110
  284.3 2.0 fusion.18
  (68 shorter events, 13.0 us)
Async XLA Ops:
  0.6 18.3 %copy-start = (s32[256,128]{1,0:T(8,128)S(1)}, s32[256,128]{1,0:T(8,128)}, u32[]{:S(2)}) copy-start(s32[256,128]{1,0:T(8,128)} %param.19) | copy-start | bytes 393220
  12.1 4.8 %copy-start.4 = (s32[2,64]{1,0:T(2,128)S(1)}, s32[2,64]{1,0:T(2,128)}, u32[]{:S(2)}) copy-start(s32[2,64]{1,0:T(2,128)} %param.17) | copy-start | bytes 1540
  12.1 4.8 %copy-start.1 = (s32[128,128]{1,0:T(8,128)S(1)}, s32[128,128]{1,0:T(8,128)}, u32[]{:S(2)}) copy-start(s32[128,128]{1,0:T(8,128)} %param.20) | copy-start | bytes 196612
  12.1 6.0 %copy-start.6 = (s32[64]{0:T(128)S(1)}, s32[64]{0:T(128)}, u32[]{:S(2)}) copy-start(s32[64]{0:T(128)} %param.23) | copy-start | bytes 772
  12.1 53.8 %all-to-all-start.3 = ((bf16[128,128,128]{2,1,0:T(8,128)(2,1)}), bf16[128,128,128]{2,1,0:T(8,128)(2,1)}, u32[]{:S(2)}, u32[]{:S(2)}) async-start(bf16[128,128,128]{2,1,0:T(8,128)(2,1)} %param.15), calls=%async_computation.3 | async-start | bytes 8388608 | tf_op jit(solution)/shard_map/all_to_all | solution.py:92
  65.9 74.1 %all-to-all-start.1 = ((s32[8,8,1]{1,2,0:T(1,128)}), s32[8,8,1]{1,2,0:T(1,128)S(1)}, u32[]{:S(2)}, u32[]{:S(2)}) async-start(s32[8,8,1]{1,2,0:T(1,128)} %bitcast.4), calls=%async_computation.1 | async-start | bytes 8192 | tf_op jit(solution)/shard_map/all_to_all | solution.py:101
  140.1 4.7 %copy-start.5 = (s32[2,32]{1,0:T(2,128)S(1)}, s32[2,32]{1,0:T(2,128)}, u32[]{:S(2)}) copy-start(s32[2,32]{1,0:T(2,128)} %param.18) | copy-start | bytes 772
  140.1 4.8 %copy-start.2 = (s32[64,128]{1,0:T(8,128)S(1)}, s32[64,128]{1,0:T(8,128)}, u32[]{:S(2)}) copy-start(s32[64,128]{1,0:T(8,128)} %param.21) | copy-start | bytes 98308
  140.1 5.9 %copy-start.7 = (s32[32]{0:T(128)S(1)}, s32[32]{0:T(128)}, u32[]{:S(2)}) copy-start(s32[32]{0:T(128)} %param.24) | copy-start | bytes 388
  140.1 53.8 %all-to-all-start.4 = ((f32[64,128,128]{2,1,0:T(8,128)}), f32[64,128,128]{2,1,0:T(8,128)}, u32[]{:S(2)}, u32[]{:S(2)}) async-start(f32[64,128,128]{2,1,0:T(8,128)} %bitcast.26), calls=%async_computation.4 | async-start | bytes 8388608 | tf_op jit(solution)/shard_map/all_to_all | solution.py:100
  193.9 16.3 %all-to-all-start = ((s32[4,8,1]{1,2,0:T(1,128)}), s32[4,8,1]{1,2,0:T(1,128)S(1)}, u32[]{:S(2)}, u32[]{:S(2)}) async-start(s32[4,8,1]{1,2,0:T(1,128)} %bitcast), calls=%async_computation | async-start | bytes 4096 | tf_op jit(solution)/shard_map/all_to_all | solution.py:107
  210.1 5.2 %copy-start.3 = (f32[8,128]{1,0:T(8,128)S(1)}, f32[8,128]{1,0:T(8,128)}, u32[]{:S(2)}) copy-start(f32[8,128]{1,0:T(8,128)} %param.25) | copy-start | bytes 12292
  210.1 74.2 %all-to-all-start.5 = ((f32[32,128,128]{2,1,0:T(8,128)}), f32[32,128,128]{2,1,0:T(8,128)S(1)}, u32[]{:S(2)}, u32[]{:S(2)}) async-start(f32[32,128,128]{2,1,0:T(8,128)} %fusion.23), calls=%async_computation.5 | async-start | bytes 4194304 | tf_op jit(solution)/shard_map/all_to_all | solution.py:106
where the time goes:
time: 289 us; the launch traced here: 288 us
  waiting for transfers between devices  91.6 us (32%)
  blocking collectives  75.2 us (26%)
  matrix products  60.4 us (21%)
  local copies, waits for them, and re-layouts  34.6 us (12%)
  starting transfers between devices  22.8 us (8%)
    psum x1, blocking collectives, per_device(): total = lax.psum(jnp.sum(vertex_weights), ('grp', 'dev'))  65.5 us
    all_to_all x1, waiting for transfers between devices, per_device(): lax.all_to_all(parts_two, 'dev', split_axis=0, concat_axis=0, tiled=True)  45.9 us
    all_to_all x1, waiting for transfers between devices, per_device(): lax.all_to_all(blocks, 'dev', split_axis=0, concat_axis=0, tiled=True)  45.7 us
    dot_general x7, matrix products, single(): jnp.einsum('gim,gij->gmj', left_hot, block_part, preferred_element_type=j...  21.3 us
    dot_general x7, matrix products, single(): jnp.einsum('gmj,gjn->gmn', halfway, right_hot, preferred_element_type=jnp...  18.7 us
    dot_general x3, matrix products, gather_sum(): jnp.dot(hot, received.reshape(received.shape[0], width * width), preferre...  18.4 us
    unnamed x18, local copies, waits for them, and re-layouts  14.5 us
    all_to_all x1, blocking collectives, per_device(): lax.all_to_all(labels, 'dev', split_axis=0, concat_axis=0, tiled=True)  9.75 us
  transfers between devices with their start and end apart: 5, of which 2 were waited for; matrix products, arithmetic and copies ran while one was open for 32% of the time, Pallas kernels for 0%

commit v1 on v0

v1 whole, which is shorter than its diff:
```python
import functools

import jax
import jax.numpy as jnp
from jax import lax
from jax.experimental import pallas as pl
from jax.experimental.pallas import tpu as pltpu
from jax.sharding import PartitionSpec as P

LEVELS = 32766.0
STEP = 16.0
FINE_STEPS = 8
HALVES = 2


def up(count, unit):
    return -(-count // unit) * unit


def one_hot(indices, width):
    rows = lax.broadcasted_iota(jnp.int32, (width, indices.shape[1]), 0)
    return jnp.where(rows == indices, 1.0, 0.0).astype(jnp.bfloat16)


def contract_lanes(left, right):
    return lax.dot_general(
        left, right, (((1,), (1,)), ((), ())), preferred_element_type=jnp.float32
    )


def compose_kernel(one_ref, two_ref, three_ref, own_ref, weights_ref, table_ref, coarse_ref):
    middle = jnp.take_along_axis(two_ref[...], one_ref[...], axis=1)
    table_ref[...] = jnp.take_along_axis(three_ref[...], middle, axis=1)
    owned, width = weights_ref.shape
    total = jnp.zeros((8, width), jnp.float32)
    for row in range(owned):
        hot = one_hot(table_ref[pl.ds(own_ref[0] + row, 1), :], width)
        value = weights_ref[row : row + 1, :]
        high = value.astype(jnp.bfloat16)
        rest = value - high.astype(jnp.float32)
        middle_part = rest.astype(jnp.bfloat16)
        low = (rest - middle_part.astype(jnp.float32)).astype(jnp.bfloat16)
        parts = jnp.concatenate(
            [high.astype(jnp.float32), middle_part.astype(jnp.float32), low.astype(jnp.float32),
             jnp.zeros((5, width), jnp.float32)], axis=0).astype(jnp.bfloat16)
        total = total + contract_lanes(parts, hot)
    coarse_ref[...] = jnp.sum(total, axis=0, keepdims=True)


def compose(match_one, match_two, match_three, weights, position):
    count, width = match_one.shape
    two = jnp.repeat(match_two, 2, axis=0)
    three = jnp.repeat(match_three, 4, axis=0)
    own = (position * weights.shape[0]).astype(jnp.int32).reshape(1)
    vmem = pl.BlockSpec(memory_space=pltpu.VMEM)
    return pl.pallas_call(
        compose_kernel,
        out_shape=(
            jax.ShapeDtypeStruct((count, width), jnp.int32),
            jax.ShapeDtypeStruct((1, width), jnp.float32),
        ),
        in_specs=[vmem, vmem, vmem, pl.BlockSpec(memory_space=pltpu.SMEM), vmem],
        out_specs=(vmem, vmem),
        name="compose",
    )(match_one, two, three, own, weights)


def encode(piece):
    top = jnp.max(jnp.abs(piece), axis=0, keepdims=True)
    exponent = jnp.ceil(jnp.log2(jnp.maximum(top, 1e-30)) * STEP)
    factor = jnp.exp2(exponent * (-1.0 / STEP)) * LEVELS
    return jnp.round(piece * factor).astype(jnp.int32).astype(jnp.int16), exponent


def encode_out(total_ref, out_ref, dest, rows):
    held = total_ref.shape[0] // out_ref.shape[0]
    width = total_ref.shape[2]
    exponents = []
    for place in range(held):
        piece = total_ref[dest * held + place]
        coded, exponent = encode(piece)
        out_ref[dest, pl.ds(place * rows, rows), :] = coded
        exponents.append(exponent)
    pad = up(held, 16) - held
    if pad:
        exponents.append(jnp.zeros((pad, width), jnp.float32))
    tail = jnp.concatenate(exponents, axis=0)
    out_ref[dest, pl.ds(held * rows, held + pad), :] = tail.astype(jnp.int32).astype(jnp.int16)


def project_kernel(per_step, halves, rows_ref, cols_ref, slots_ref, table_ref, blocks_ref, *refs):
    outs, totals = refs[:halves], refs[halves:]
    step = pl.program_id(0)
    width = blocks_ref.shape[2]
    part = width // halves

    @pl.when(step == 0)
    def _():
        for total_ref in totals:
            total_ref[...] = jnp.zeros_like(total_ref)

    for place in range(per_step):
        k = step * per_step + place
        left = one_hot(table_ref[pl.ds(rows_ref[k], 1), :], width)
        right = one_hot(table_ref[pl.ds(cols_ref[k], 1), :], width)
        half = jnp.dot(left, blocks_ref[place], preferred_element_type=jnp.float32)
        high = half.astype(jnp.bfloat16)
        low = (half - high.astype(jnp.float32)).astype(jnp.bfloat16)
        both = contract_lanes(
            jnp.concatenate([high, low], axis=1), jnp.concatenate([right, right], axis=1)
        )
        slot = slots_ref[k]
        for h, total_ref in enumerate(totals):
            total_ref[slot] += both[h * part : (h + 1) * part]

    @pl.when(step == pl.num_programs(0) - 1)
    def _():
        for total_ref, out_ref in zip(totals, outs):
            lax.fori_loop(
                0, out_ref.shape[0],
                lambda dest, _: (encode_out(total_ref, out_ref, dest, part), 0)[1], 0)


def coded_rows(held, rows):
    return held * rows + up(held, 16)


def project_sum(blocks, rows, cols, slots, table, count, dests, halves):
    number, width = blocks.shape[:2]
    per_step = number // FINE_STEPS
    part = width // halves
    shape = (dests, coded_rows(count // dests, part), width)
    return pl.pallas_call(
        functools.partial(project_kernel, per_step, halves),
        grid_spec=pltpu.PrefetchScalarGridSpec(
            num_scalar_prefetch=3,
            grid=(FINE_STEPS,),
            in_specs=[
                pl.BlockSpec(table.shape, lambda s, *_: (0, 0)),
                pl.BlockSpec((per_step, width, width), lambda s, *_: (s, 0, 0)),
            ],
            out_specs=[pl.BlockSpec(shape, lambda s, *_: (0, 0, 0))] * halves,
            scratch_shapes=[pltpu.VMEM((count, part, width), jnp.float32)] * halves,
        ),
        out_shape=[jax.ShapeDtypeStruct(shape, jnp.int16)] * halves,
        compiler_params=pltpu.CompilerParams(vmem_limit_bytes=48 * 1024 * 1024),
        name="project_sum",
    )(rows, cols, slots, table, blocks)


def merge_kernel(held, rows, coded, slots_ref, in_ref, out_ref, *scratch):
    total_ref = scratch[0] if coded else out_ref
    source = pl.program_id(0)

    @pl.when(source == 0)
    def _():
        total_ref[...] = jnp.zeros_like(total_ref)

    tail = in_ref[0, pl.ds(held * rows, up(held, 16)), :].astype(jnp.int32).astype(jnp.float32)
    factors = jnp.exp2(tail * (1.0 / STEP)) * (1.0 / LEVELS)
    for place in range(held):
        piece = in_ref[0, pl.ds(place * rows, rows), :].astype(jnp.int32).astype(jnp.float32)
        slot = slots_ref[source * held + place]
        total_ref[slot] += piece * factors[place : place + 1, :]

    if coded:
        @pl.when(source == pl.num_programs(0) - 1)
        def _():
            lax.fori_loop(
                0, out_ref.shape[0],
                lambda dest, _: (encode_out(total_ref, out_ref, dest, rows), 0)[1], 0)


def merge(received, slots, count, rows, dests):
    sources, _, width = received.shape
    held = slots.shape[0] // sources
    if dests:
        shape, kind = (dests, coded_rows(count // dests, rows), width), jnp.int16
        scratch = [pltpu.VMEM((count, rows, width), jnp.float32)]
    else:
        shape, kind, scratch = (count, rows, width), jnp.float32, []
    return pl.pallas_call(
        functools.partial(merge_kernel, held, rows, bool(dests)),
        grid_spec=pltpu.PrefetchScalarGridSpec(
            num_scalar_prefetch=1,
            grid=(sources,),
            in_specs=[pl.BlockSpec((1,) + received.shape[1:], lambda s, *_: (s, 0, 0))],
            out_specs=pl.BlockSpec(shape, lambda s, *_: (0, 0, 0)),
            scratch_shapes=scratch,
        ),
        out_shape=jax.ShapeDtypeStruct(shape, kind),
        compiler_params=pltpu.CompilerParams(vmem_limit_bytes=40 * 1024 * 1024),
        name="merge",
    )(slots, received)


def exchange(array, axis):
    return lax.all_to_all(array, axis, split_axis=0, concat_axis=0, tiled=True)


def per_device(
    blocks, ids_one, ids_two, ids_three, match_one, match_two, match_three,
    target_one, target_two, target_three, vertex_weights,
):
    fine = blocks.shape[0]
    devs, groups = lax.axis_size("dev"), lax.axis_size("grp")
    share, share_two = fine // devs, fine // 2 // devs

    fine_in = exchange(blocks, "dev")
    labels = jnp.concatenate(
        [ids_one[0].reshape(devs, share), ids_one[1].reshape(devs, share),
         target_one.reshape(devs, share), target_two.reshape(devs, share_two)], axis=1
    ).astype(jnp.float32)
    own_sum = jnp.full((devs, 1), jnp.sum(vertex_weights))
    arrived = exchange(jnp.concatenate([labels, own_sum], axis=1), "dev")
    whole = arrived[:, : 3 * share + share_two].astype(jnp.int32)
    group_sum = jnp.sum(arrived[:, -1])
    arrived_three = exchange(
        jnp.concatenate(
            [target_three.reshape(groups, -1).astype(jnp.float32), jnp.full((groups, 1), group_sum)],
            axis=1), "grp")
    total = jnp.sum(arrived_three[:, -1])
    slots_three = arrived_three[:, :-1].astype(jnp.int32).reshape(-1)
    rows = whole[:, :share].reshape(-1)
    cols = whole[:, share : 2 * share].reshape(-1)
    slots = whole[:, 2 * share : 3 * share].reshape(-1)
    slots_two = whole[:, 3 * share :].reshape(-1)

    position = lax.axis_index(("grp", "dev"))
    table, weights_three = compose(match_one, match_two, match_three, vertex_weights, position)
    vertices = lax.axis_size(("grp", "dev")) * weights_three.shape[1]
    rel_weight = weights_three * vertices / total

    part = blocks.shape[1] // HALVES
    pieces = project_sum(fine_in, rows, cols, slots, table, fine // 2, devs, HALVES)
    received = [exchange(piece, "dev") for piece in pieces]
    seconds = [merge(piece, slots_two, fine // 4, part, groups) for piece in received]
    thirds = [exchange(piece, "grp") for piece in seconds]
    finals = [merge(piece, slots_three, fine // 8, part, 0) for piece in thirds]
    return (jnp.concatenate(finals, axis=1), rel_weight)


def solution(mesh):
    whole = P(("grp", "dev"))
    return jax.shard_map(
        per_device,
        mesh=mesh,
        in_specs=(
            P(("grp", "dev"), None, None),
            P(None, ("grp", "dev")),
            P(None, ("grp", "dev")),
            P(None, ("grp", "dev")),
            P(),
            P(),
            P(),
            whole,
            whole,
            whole,
            P(("grp", "dev"), None),
        ),
        out_specs=(P(("grp", "dev"), None, None), P(("grp", "dev"), None)),
        check_vma=False,
    )
```

time: 289 us -> 165 us (0.57)
  matrix products: 60.4 us -> 0 us
  blocking collectives: 75.2 us -> 27.7 us
  local copies, waits for them, and re-layouts: 34.6 us -> 7.2 us
  Pallas kernels: 0 us -> 23.8 us
  waiting for transfers between devices: 91.6 us -> 76.3 us
    psum x1 -> x0, blocking collectives: 65.5 us -> none  [per_device(): total = lax.psum(jnp.sum(vertex_weights), ('grp', 'dev'))]
    dot_general x20 -> x0, matrix products: 60.4 us -> none  [the longest x7 21.3 us: single(): jnp.einsum('gim,gij->gmj', left_hot, block_part, preferred_element_type=j...]
    pallas_call x0 -> x6, Pallas kernels: none -> 23.8 us  [the longest x1 15.6 us: project_sum(): pl.pallas_call(functools.partial(project_kernel, per_step, halves), grid_...]
    all_to_all x1 -> x2, blocking collectives: 9.75 us -> 27.7 us  [exchange(): return lax.all_to_all(array, axis, split_axis=0, concat_axis=0, tiled=True)]
    all_to_all x5, waiting for transfers between devices: 91.6 us -> 76.3 us  [exchange(): return lax.all_to_all(array, axis, split_axis=0, concat_axis=0, tiled=True)]
    unnamed x18 -> x10, local copies, waits for them, and re-layouts: 14.5 us -> 0.92 us
    dot_general x1 -> x0, local copies, waits for them, and re-layouts: 9 us -> none  [gather_sum(): jnp.dot(hot, received.reshape(received.shape[0], width * width), preferre...]
    gather x6 -> x0, local copies, waits for them, and re-layouts: 3.63 us -> none  [the longest x3 1.82 us: project(): row_map = table[pair_ids[0]]]
  transfers between devices with their start and end apart: 5 -> 5, of which waited for: 2 -> 4; matrix products, arithmetic and copies ran while one was open for 32% -> 4% of each run, Pallas kernels for 0% -> 14%
where the time goes in v1:
time: 165 us; the launch traced here: 162 us
  waiting for transfers between devices  76.3 us (46%)
  blocking collectives  27.7 us (17%)
  Pallas kernels  23.8 us (14%)
  starting transfers between devices  21.7 us (13%)
  local copies, waits for them, and re-layouts  7.2 us (4%)
  other arithmetic  4.93 us (3%)
    all_to_all x5, waiting for transfers between devices, exchange(): return lax.all_to_all(array, axis, split_axis=0, concat_axis=0, tiled=True)  76.3 us
    all_to_all x2, blocking collectives, exchange(): return lax.all_to_all(array, axis, split_axis=0, concat_axis=0, tiled=True)  27.7 us
    all_to_all x5, starting transfers between devices, exchange(): return lax.all_to_all(array, axis, split_axis=0, concat_axis=0, tiled=True)  21.7 us
    pallas_call x1, Pallas kernels, project_sum(): pl.pallas_call(functools.partial(project_kernel, per_step, halves), grid_...  15.6 us
    pallas_call x4, Pallas kernels, merge(): pl.pallas_call(functools.partial(merge_kernel, held, rows, bool(dests)),...  6.05 us
  transfers between devices with their start and end apart: 5, of which 4 were waited for; matrix products, arithmetic and copies ran while one was open for 4% of the time, Pallas kernels for 14%

profile of v1, /device:TPU:0, one launch (start us, length us, event | category | flops | bytes accessed | tf_op | source)
XLA Modules:
  0.0 162.3 jit_solution(8221814326813599339)
XLA Ops:
  0.6 0.8 slice_reduce_fusion.3
  1.6 0.7 reshape.40
  2.3 0.7 reshape.41
  3.0 1.3 reduce_sum.27
  4.4 0.6 concatenate.13
  5.1 9.7 %all_to_all.49 = f32[8,1,57]{2,1,0:T(1,128)S(1)} all-to-all(f32[8,1,57]{2,1,0:T(1,128)S(1)} %bitcast.17), channel_id=1, replica_groups=mesh['grp'=4,'dev'=8] {'dev'}, dimensions={0} | all-to-all | bytes 3648 | tf_op jit(solution)/shard_map/all_to_all | solution.py:198
  14.8 4.7 %all-to-all-start.2 = ((bf16[128,128,128]{2,1,0:T(8,128)(2,1)}), bf16[128,128,128]{2,1,0:T(8,128)(2,1)}, u32[]{:S(2)}, u32[]{:S(2)}) async-start(bf16[128,128,128]{2,1,0:T(8,128)(2,1)} %param.11), calls=%async_computation.2 | async-start | bytes 8388608 | tf_op jit(solution)/shard_map/all_to_all | solution.py:198
  19.5 0.1 convert_element_type.16
  19.6 0.7 broadcast_in_dim.8
  20.3 0.7 broadcast_in_dim.9
  20.9 2.1 %compose.1 = (s32[256,128]{1,0:T(8,128)}, f32[1,128]{1,0:T(1,128)}) custom-call(s32[256,128]{1,0:T(8,128)} %one_ref.1, s32[256,128]{1,0:T(8,128)} %bitcast.12, s32[256,128]{1,0:T(8,128)} %bitcast.11, s32[1]{0:T(128)} %bitcast.8.own_ref, f32[8,128]{1,0:T(8,128)} %weights_ref.1), custom_call_target="tpu_custom_call" | custom-call | tf_op jit(solution)/shard_map/compose/pallas_call | solution.py:56
  23.3 0.7 slice_reduce_fusion
  24.0 1.2 concatenate.14
  25.2 43.3 %all-to-all-done.2.blocks_ref = bf16[128,128,128]{2,1,0:T(8,128)(2,1)} async-done(((bf16[128,128,128]{2,1,0:T(8,128)(2,1)}), bf16[128,128,128]{2,1,0:T(8,128)(2,1)}, u32[]{:S(2)}, u32[]{:S(2)}) %all-to-all-start.2) | async-done | bytes 4194336 | tf_op jit(solution)/shard_map/all_to_all | solution.py:198
  68.5 4.9 %all-to-all-start.1 = ((f32[4,1,9]{2,1,0:T(1,128)}), f32[4,1,9]{2,1,0:T(1,128)S(1)}, u32[]{:S(2)}, u32[]{:S(2)}) async-start(f32[4,1,9]{2,1,0:T(1,128)} %bitcast.4), calls=%async_computation.1 | async-start | bytes 4096 | tf_op jit(solution)/shard_map/all_to_all | solution.py:198
  73.5 0.9 copy-done
  74.4 15.6 %project_sum.1 = (s16[8,528,128]{2,1,0:T(8,128)(2,1)S(1)}, s16[8,528,128]{2,1,0:T(8,128)(2,1)}) custom-call(s32[128]{0:T(128)S(1)} %reshape.44.rows_ref, s32[128]{0:T(128)S(1)} %reshape.45.cols_ref, s32[128]{0:T(128)S(1)} %reshape.46.slots_ref, s32[256,128]{1,0:T(8,128)S(1)} %copy-done, bf16[128,128,128]{2,1,0:T(8,128)(2,1)} %all-to-all-done.2.blocks_ref), custom_call_target="tpu_custom_call" | custom-call | tf_op jit(solution)/shard_map/project_sum/pallas_call | solution.py:133
  90.0 18.1 %all_to_all.50.in_ref = s16[8,528,128]{2,1,0:T(8,128)(2,1)S(1)} all-to-all(s16[8,528,128]{2,1,0:T(8,128)(2,1)S(1)} %get-tuple-element.7), channel_id=1, replica_groups=mesh['grp'=4,'dev'=8] {'dev'}, dimensions={0} | all-to-all | bytes 2162688 | tf_op jit(solution)/shard_map/all_to_all | solution.py:198
  108.0 3.6 %all-to-all-start.5 = ((s16[8,528,128]{2,1,0:T(8,128)(2,1)}), s16[8,528,128]{2,1,0:T(8,128)(2,1)S(1)}, u32[]{:S(2)}, u32[]{:S(2)}) async-start(s16[8,528,128]{2,1,0:T(8,128)(2,1)} %get-tuple-element.8), calls=%async_computation.5 | async-start | bytes 2162688 | tf_op jit(solution)/shard_map/all_to_all | solution.py:198
  111.8 2.2 %merge.4 = s16[4,528,128]{2,1,0:T(8,128)(2,1)} custom-call(s32[64]{0:T(128)S(1)} %reshape.43.slots_ref, s16[8,528,128]{2,1,0:T(8,128)(2,1)S(1)} %all_to_all.50.in_ref), custom_call_target="tpu_custom_call" | custom-call | tf_op jit(solution)/shard_map/merge/pallas_call | solution.py:182
  113.9 13.3 %all-to-all-done.5.in_ref = s16[8,528,128]{2,1,0:T(8,128)(2,1)S(1)} async-done(((s16[8,528,128]{2,1,0:T(8,128)(2,1)}), s16[8,528,128]{2,1,0:T(8,128)(2,1)S(1)}, u32[]{:S(2)}, u32[]{:S(2)}) %all-to-all-start.5) | async-done | bytes 1081376 | tf_op jit(solution)/shard_map/all_to_all | solution.py:198
  127.3 5.1 %all-to-all-start.4 = ((s16[4,528,128]{2,1,0:T(8,128)(2,1)}), s16[4,528,128]{2,1,0:T(8,128)(2,1)S(1)}, u32[]{:S(2)}, u32[]{:S(2)}) async-start(s16[4,528,128]{2,1,0:T(8,128)(2,1)} %merge.4), calls=%async_computation.4 | async-start | bytes 1081344 | tf_op jit(solution)/shard_map/all_to_all | solution.py:198
  132.4 2.2 %merge.6 = s16[4,528,128]{2,1,0:T(8,128)(2,1)} custom-call(s32[64]{0:T(128)S(1)} %reshape.43.slots_ref, s16[8,528,128]{2,1,0:T(8,128)(2,1)S(1)} %all-to-all-done.5.in_ref), custom_call_target="tpu_custom_call" | custom-call | tf_op jit(solution)/shard_map/merge/pallas_call | solution.py:182
  134.5 9.8 %all-to-all-done.4.in_ref = s16[4,528,128]{2,1,0:T(8,128)(2,1)S(1)} async-done(((s16[4,528,128]{2,1,0:T(8,128)(2,1)}), s16[4,528,128]{2,1,0:T(8,128)(2,1)S(1)}, u32[]{:S(2)}, u32[]{:S(2)}) %all-to-all-start.4) | async-done | bytes 540704 | tf_op jit(solution)/shard_map/all_to_all | solution.py:198
  144.4 3.5 %all-to-all-start.6 = ((s16[4,528,128]{2,1,0:T(8,128)(2,1)}), s16[4,528,128]{2,1,0:T(8,128)(2,1)S(1)}, u32[]{:S(2)}, u32[]{:S(2)}) async-start(s16[4,528,128]{2,1,0:T(8,128)(2,1)} %merge.6), calls=%async_computation.6 | async-start | bytes 1081344 | tf_op jit(solution)/shard_map/all_to_all | solution.py:198
  147.9 0.1 reshape.42.slots_ref
  147.9 0.7 slice_reduce_fusion.1
  148.6 1.1 multiply_divide_fusion
  149.8 0.8 merge.5
  150.6 9.8 %all-to-all-done.6.in_ref = s16[4,528,128]{2,1,0:T(8,128)(2,1)S(1)} async-done(((s16[4,528,128]{2,1,0:T(8,128)(2,1)}), s16[4,528,128]{2,1,0:T(8,128)(2,1)S(1)}, u32[]{:S(2)}, u32[]{:S(2)}) %all-to-all-start.6) | async-done | bytes 540704 | tf_op jit(solution)/shard_map/all_to_all | solution.py:198
  160.4 0.8 merge.7
  161.3 1.1 pad_maximum_fusion
  (22 shorter events, 0.7 us)
Async XLA Ops:
  14.7 4.7 %copy-start.3 = (s32[32]{0:T(128)S(1)}, s32[32]{0:T(128)}, u32[]{:S(2)}) copy-start(s32[32]{0:T(128)} %param.18) | copy-start | bytes 388
  14.8 4.8 %copy-start.1 = (s32[128,128]{1,0:T(8,128)S(1)}, s32[128,128]{1,0:T(8,128)}, u32[]{:S(2)}) copy-start(s32[128,128]{1,0:T(8,128)} %param.14) | copy-start | bytes 196612
  14.8 5.5 %copy-start.2 = (s32[64,128]{1,0:T(8,128)S(1)}, s32[64,128]{1,0:T(8,128)}, u32[]{:S(2)}) copy-start(s32[64,128]{1,0:T(8,128)} %param.15) | copy-start | bytes 98308
  14.8 53.8 %all-to-all-start.2 = ((bf16[128,128,128]{2,1,0:T(8,128)(2,1)}), bf16[128,128,128]{2,1,0:T(8,128)(2,1)}, u32[]{:S(2)}, u32[]{:S(2)}) async-start(bf16[128,128,128]{2,1,0:T(8,128)(2,1)} %param.11), calls=%async_computation.2 | async-start | bytes 8388608 | tf_op jit(solution)/shard_map/all_to_all | solution.py:198
  68.5 21.4 %all-to-all-start.1 = ((f32[4,1,9]{2,1,0:T(1,128)}), f32[4,1,9]{2,1,0:T(1,128)S(1)}, u32[]{:S(2)}, u32[]{:S(2)}) async-start(f32[4,1,9]{2,1,0:T(1,128)} %bitcast.4), calls=%async_computation.1 | async-start | bytes 4096 | tf_op jit(solution)/shard_map/all_to_all | solution.py:198
  73.5 0.9 copy-start
  108.0 19.2 %all-to-all-start.5 = ((s16[8,528,128]{2,1,0:T(8,128)(2,1)}), s16[8,528,128]{2,1,0:T(8,128)(2,1)S(1)}, u32[]{:S(2)}, u32[]{:S(2)}) async-start(s16[8,528,128]{2,1,0:T(8,128)(2,1)} %get-tuple-element.8), calls=%async_computation.5 | async-start | bytes 2162688 | tf_op jit(solution)/shard_map/all_to_all | solution.py:198
  127.3 17.1 %all-to-all-start.4 = ((s16[4,528,128]{2,1,0:T(8,128)(2,1)}), s16[4,528,128]{2,1,0:T(8,128)(2,1)S(1)}, u32[]{:S(2)}, u32[]{:S(2)}) async-start(s16[4,528,128]{2,1,0:T(8,128)(2,1)} %merge.4), calls=%async_computation.4 | async-start | bytes 1081344 | tf_op jit(solution)/shard_map/all_to_all | solution.py:198
  132.4 16.3 %copy-start.4 = (f32[1,128]{1,0:T(1,128)S(1)}, f32[1,128]{1,0:T(1,128)}, u32[]{:S(2)}) copy-start(f32[1,128]{1,0:T(1,128)} %get-tuple-element.9) | copy-start | bytes 1540
  144.4 16.1 %all-to-all-start.6 = ((s16[4,528,128]{2,1,0:T(8,128)(2,1)}), s16[4,528,128]{2,1,0:T(8,128)(2,1)S(1)}, u32[]{:S(2)}, u32[]{:S(2)}) async-start(s16[4,528,128]{2,1,0:T(8,128)(2,1)} %merge.6), calls=%async_computation.6 | async-start | bytes 1081344 | tf_op jit(solution)/shard_map/all_to_all | solution.py:198
